TPU v7x, 256 devices: a whole 4x4x8 slice. The times are simulated.
256 devices in a mesh: pop: 32 (over z, y_lo, core), tp: 8 (over y_hi, x).
Axes of the slice: x: 4, y: 4 (y_hi: 2, y_lo: 2; y = y_hi * 2 + y_lo), z: 8, core: 2. Of those that a mesh axis runs over, the one named last changes fastest.
Arguments:
- tokens: bfloat16 [32, 512, 1792], P('pop', None, 'tp'), may hold values from -6 to 6
- weight: bfloat16 [32, 1792, 7168], P('pop', 'tp'), may hold values from -0.125 to 0.125
- momentum: bfloat16 [32, 1792, 7168], P('pop', 'tp'), may hold values from -6 to 6
- cotangent: bfloat16 [32, 512, 7168], P('pop', None, 'tp'), may hold values from -0.5 to 0.5
- assignment: int32 [8, 2], replicated, may hold values from 0 to 31, as said below
- lr_index: int32 [32], replicated, may hold values from 0 to 7
- rates: float32 [8], replicated, may hold values from 0.01 to 0.1
Outputs:
- activation: bfloat16 [32, 512, 7168], P('pop', None, 'tp')
- new_weight: bfloat16 [32, 1792, 7168], P('pop', 'tp')
Inputs may be any that keep to these rules, and one draw needn't show every extreme that they name: `assignment`: column 0 names 8 distinct members; column 1 names exactly 2 distinct members, each in some row, none of them in column 0.
All inputs are finite; a program needn't handle non-finite values.
Results may differ from a plain program's by a relative error of at most 0.015.
Values may be sent and summed in bfloat16 or wider, within the bound.
No kernel may reach another device: no remote copies, remote signals or barrier semaphores. Data moves between devices by JAX's collectives and lax.ppermute only.
A program may use at most 192 MiB of HBM per device.

v0:
```python
import jax
import jax.numpy as jnp
from jax import lax
from jax.sharding import PartitionSpec as P


def side_by_side(arrays, axis, split_dim, concat_dim, along):
    both = jnp.concatenate(arrays, axis=along)
    filled, at, done = (
        lax.all_to_all(both, axis, split_axis=split_dim, concat_axis=concat_dim, tiled=True),
        0,
        [],
    )
    for a in arrays:
        done.append(lax.slice_in_dim(filled, at, at + a.shape[along], axis=along))
        at += a.shape[along]
    return tuple(done)


def gelu_tanh(value):
    return jax.nn.gelu(value, approximate=True)


def activate(hidden, cot_block):
    active, pullback = jax.vjp(gelu_tanh, hidden)
    grad_hidden = pullback(cot_block.astype(jnp.float32))[0].astype(jnp.bfloat16)
    return (active.astype(jnp.bfloat16), grad_hidden)


def local(tokens, weight, momentum, cotangent, assignment, lr_index, rates):
    members = lax.axis_size("pop")
    me = lax.axis_index("pop")
    member_ids = jnp.arange(members, dtype=jnp.int32)
    hit = assignment[:, 0][None, :] == member_ids[:, None]
    source_all = jnp.where(
        jnp.any(hit, axis=1),
        jnp.sum(jnp.where(hit, assignment[:, 1][None, :], 0), axis=1),
        member_ids,
    )
    my_index = jnp.sum(jnp.where(member_ids == me, lr_index, 0))
    rate_ids = jnp.arange(rates.shape[0], dtype=jnp.int32)
    my_rate = jnp.sum(jnp.where(rate_ids == my_index, rates, 0.0))
    flat_weight = weight.reshape(members, -1)
    flat_momentum = momentum.reshape(members, -1)
    held = side_by_side((flat_weight, flat_momentum), "pop", 0, 0, 1)
    picked = (held[0][source_all], held[1][source_all])
    returned = side_by_side((picked[0], picked[1]), "pop", 0, 0, 1)
    taken_weight = returned[0].reshape(weight.shape)[0]
    taken_momentum = returned[1].reshape(momentum.shape)[0]
    inputs = tokens[0]
    partial_value = jnp.dot(inputs, taken_weight, preferred_element_type=jnp.float32)
    hidden_share = lax.psum_scatter(
        partial_value.astype(jnp.bfloat16), "tp", scatter_dimension=1, tiled=True
    ).astype(jnp.float32)
    activation, grad_share = activate(hidden_share, cotangent[0])
    grad_hidden = lax.all_gather(grad_share, "tp", axis=1, tiled=True)
    grad_weight = lax.dot_general(
        inputs, grad_hidden, (((0,), (0,)), ((), ())), preferred_element_type=jnp.float32
    )
    new_momentum = 0.9 * taken_momentum.astype(jnp.float32) + grad_weight
    updated = (taken_weight.astype(jnp.float32) - my_rate * new_momentum).astype(jnp.bfloat16)
    return (activation[None], updated[None])


def solution(mesh):
    placed = (
        P("pop", None, "tp"),
        P("pop", "tp", None),
        P("pop", "tp", None),
        P("pop", None, "tp"),
        P(),
        P(),
        P(),
    )
    return jax.shard_map(
        local,
        mesh=mesh,
        in_specs=placed,
        out_specs=(P("pop", None, "tp"), P("pop", "tp", None)),
        check_vma=False,
    )
```

profile of v0, /device:TPU:1, one launch (start us, length us, event | category | flops | bytes accessed | tf_op | source)
XLA Modules:
  0.0 701.8 jit_solution(3552922835400282896)
XLA Ops:
  7.2 0.0 copy-start
  7.2 5.6 reshape.46
  12.8 6.7 reshape.45
  19.5 5.0 maximum_bitcast_fusion
  24.5 0.5 broadcast.61
  25.0 9.3 %reduce = bf16[32,100352]{1,0:T(8,128)(2,1)} reduce(bf16[32,1,100352]{2,0,1:T(8,128)(2,1)} %maximum_bitcast_fusion, bf16[]{:T(256)} %broadcast.61), dimensions={1}, to_apply=%copy.18.reduce_sub_computation | reduce | bytes 12845058 | tf_op jit(solution)/shard_map/all_to_all | solution.py:10
  34.4 8.9 %reshape.64 = bf16[32,2,50176]{2,1,0:T(2,128)(2,1)} reshape(bf16[32,100352]{1,0:T(8,128)(2,1)} %reduce) | data formatting | bytes 12845056
  43.2 0.0 copy-start.1
  43.2 11.3 %all-to-all-start = ((bf16[32,2,50176]{2,1,0:T(2,128)(2,1)}), bf16[32,2,50176]{2,1,0:T(2,128)(2,1)}, u32[]{:S(2)}, u32[]{:S(2)}) async-start(bf16[32,2,50176]{2,1,0:T(2,128)(2,1)} %reshape.64), calls=%async_computation | async-start | bytes 12845056 | tf_op jit(solution)/shard_map/all_to_all | solution.py:10
  54.5 0.0 reduce-scatter.2.cloned.1.call-start
  54.6 0.0 copy-done.1
  54.6 0.1 fusion.20
  54.7 0.1 select_reduce_fusion
  54.8 141.1 %all-to-all-done = bf16[32,2,50176]{2,1,0:T(2,128)(2,1)} async-done(((bf16[32,2,50176]{2,1,0:T(2,128)(2,1)}), bf16[32,2,50176]{2,1,0:T(2,128)(2,1)}, u32[]{:S(2)}, u32[]{:S(2)}) %all-to-all-start) | async-done | bytes 6422560 | tf_op jit(solution)/shard_map/all_to_all | solution.py:10
  195.9 21.7 %reshape.65 = bf16[32,1,100352]{2,1,0:T(2,128)(2,1)} reshape(bf16[32,2,50176]{2,1,0:T(2,128)(2,1)} %all-to-all-done) | data formatting | bytes 12845056
  217.7 11.0 %copy.27 = bf16[32,1,100352]{2,0,1:T(8,128)(2,1)} copy(bf16[32,1,100352]{2,1,0:T(2,128)(2,1)} %reshape.65) | data formatting | bytes 12845056
  228.7 5.0 fusion.24
  233.7 9.4 %gather_fusion.1 = bf16[32,50176]{1,0:T(8,128)(2,1)} fusion(bf16[32,50176]{1,0:T(8,128)(2,1)} %get-tuple-element.11, s32[1024]{0:T(1024)S(1)} %pad_clamp_fusion), kind=kCustom, calls=%fused_computation.1 | custom fusion | bytes 6422656 | tf_op jit(solution)/shard_map/gather | solution.py:46
  243.0 4.3 gather_fusion
  247.4 6.0 maximum_bitcast_fusion.1
  253.4 9.5 %reduce.1 = bf16[32,100352]{1,0:T(8,128)(2,1)} reduce(bf16[32,1,100352]{2,0,1:T(8,128)(2,1)} %maximum_bitcast_fusion.1, bf16[]{:T(256)} %broadcast.61), dimensions={1}, to_apply=%copy.19.reduce_sub_computation | reduce | bytes 12845058 | tf_op jit(solution)/shard_map/all_to_all | solution.py:10
  262.9 8.9 %reshape.66 = bf16[32,2,50176]{2,1,0:T(2,128)(2,1)} reshape(bf16[32,100352]{1,0:T(8,128)(2,1)} %reduce.1) | data formatting | bytes 12845056
  271.7 151.7 %all_to_all.24 = bf16[32,2,50176]{2,1,0:T(2,128)(2,1)} all-to-all(bf16[32,2,50176]{2,1,0:T(2,128)(2,1)} %reshape.66), channel_id=1, replica_groups=mesh['pop'=32,'tp'=8] {'pop'}, dimensions={0} | all-to-all | bytes 12845056 | tf_op jit(solution)/shard_map/all_to_all | solution.py:10
  423.5 21.3 %reshape.67 = bf16[32,1,100352]{2,1,0:T(2,128)(2,1)} reshape(bf16[32,2,50176]{2,1,0:T(2,128)(2,1)} %all_to_all.24) | data formatting | bytes 12845056
  444.7 11.1 %copy.26 = bf16[32,1,100352]{2,0,1:T(8,128)(2,1)} copy(bf16[32,1,100352]{2,1,0:T(2,128)(2,1)} %reshape.67) | data formatting | bytes 12845056
  455.8 3.8 slice.30
  459.6 5.5 squeeze_reshape.4
  465.1 0.0 copy-done
  465.1 5.1 fusion
  470.3 0.0 reduce-scatter.2.cloned.1.call-update
  470.3 0.0 copy-start.2
  470.3 0.0 copy-start.3
  470.3 0.0 all-gather.2.cloned.1.call-start
  470.4 2.4 copy.20
  472.8 105.8 %reduce-scatter.2.cloned.1.call-done = bf16[512,896]{0,1:T(8,128)(2,1)} async-done(((bf16[512,7168]{0,1:T(8,128)(2,1)}), bf16[512,896]{0,1:T(8,128)(2,1)}) %reduce-scatter.2.cloned.1.call-update) | async-done | bytes 917520 | tf_op jit(solution)/shard_map/reduce_scatter | solution.py:52
  578.6 4.1 fusion.9
  582.8 0.0 all-gather.2.cloned.1.call-update
  582.8 0.0 copy-done.2
  582.8 0.6 fusion.21
  583.4 0.0 copy-done.3
  583.4 1.3 fusion.22
  584.7 5.0 convert_multiply_fusion
  589.7 6.3 mul.66
  596.1 2.3 copy.21
  598.4 86.8 %all-gather.2.cloned.1.call-done = bf16[512,7168]{0,1:T(8,128)(2,1)} async-done(((bf16[512,896]{0,1:T(8,128)(2,1)}), bf16[512,7168]{0,1:T(8,128)(2,1)}) %all-gather.2.cloned.1.call-update) | async-done | bytes 7340048 | tf_op jit(solution)/shard_map/all_gather | solution.py:56
  685.2 9.6 %fusion.5 = bf16[1,224,7168]{2,1,0:T(8,128)(2,1)} fusion(f32[224,7168]{1,0:T(8,128)} %mul.66, bf16[512,7168]{0,1:T(8,128)(2,1)} %all-gather.2.cloned.1.call-done, bf16[224,7168]{1,0:T(8,128)(2,1)S(1)} %squeeze_reshape.4, f32[]{:T(128)} %fusion.22, bf16[1,512,224]{1,2,0:T(8,128)(2,1)S(1)} %copy-done), kind=kOutput, calls=%fused_computation.9 | convolution fusion | flops 1652195328 | bytes 20414468 | tf_op jit(solution)/shard_map/dot_general | solution.py:57
  (3 shorter events, 0.0 us)
Async XLA Ops:
  7.2 458.0 %copy-start = (bf16[1,512,224]{1,2,0:T(8,128)(2,1)S(1)}, bf16[1,512,224]{1,2,0:T(8,128)(2,1)}, u32[]{:S(2)}) copy-start(bf16[1,512,224]{1,2,0:T(8,128)(2,1)} %param.7) | copy-start | bytes 688132
  43.2 11.4 %copy-start.1 = (s32[8,2]{0,1:T(2,128)S(1)}, s32[8,2]{0,1:T(2,128)}, u32[]{:S(2)}) copy-start(s32[8,2]{0,1:T(2,128)} %param.11) | copy-start | bytes 196
  43.2 152.7 %all-to-all-start = ((bf16[32,2,50176]{2,1,0:T(2,128)(2,1)}), bf16[32,2,50176]{2,1,0:T(2,128)(2,1)}, u32[]{:S(2)}, u32[]{:S(2)}) async-start(bf16[32,2,50176]{2,1,0:T(2,128)(2,1)} %reshape.64), calls=%async_computation | async-start | bytes 12845056 | tf_op jit(solution)/shard_map/all_to_all | solution.py:10
  54.5 524.1 %reduce-scatter.2.cloned.1.call-start = ((), (), s32[]{:S(2)}) async-start(), calls=%async_computation.3 | async-start | bytes 8257536 | tf_op jit(solution)/shard_map/reduce_scatter | solution.py:52
  470.3 112.5 %copy-start.2 = (s32[32]{0:T(128)S(1)}, s32[32]{0:T(128)}, u32[]{:S(2)}) copy-start(s32[32]{0:T(128)} %param.12) | copy-start | bytes 388
  470.3 113.1 %copy-start.3 = (f32[8]{0:T(128)S(1)}, f32[8]{0:T(128)}, u32[]{:S(2)}) copy-start(f32[8]{0:T(128)} %param.13) | copy-start | bytes 100
  470.3 214.8 %all-gather.2.cloned.1.call-start = ((), (), s32[]{:S(2)}) async-start(), calls=%async_computation.4 | async-start | bytes 8257536 | tf_op jit(solution)/shard_map/all_gather | solution.py:56
Sparse Core Ops, SparseCore 0:
  470.4 108.1 reduce-scatter.1
  582.9 102.2 all-gather.1
where the time goes:
time: 710 us; the launch traced here: 702 us
  waiting for transfers between devices  334 us (47%)
  blocking collectives  152 us (21%)
  local copies, waits for them, and re-layouts  135 us (19%)
  other arithmetic  41.1 us (6%)
  matrix products  14.7 us (2%)
  between operations  14.4 us (2%)
  starting transfers between devices  11.4 us (2%)
    all_to_all x1, blocking collectives, side_by_side(): lax.all_to_all(both, axis, split_axis=split_dim, concat_axis=concat_dim,...  152 us
    all_to_all x1, waiting for transfers between devices, side_by_side(): lax.all_to_all(both, axis, split_axis=split_dim, concat_axis=concat_dim,...  141 us
    reduce_scatter x1, waiting for transfers between devices, local(): lax.psum_scatter(partial_value.astype(jnp.bfloat16), 'tp', scatter_dimens...  106 us
    unnamed x16, local copies, waits for them, and re-layouts  87.6 us
    all_gather x1, waiting for transfers between devices, local(): grad_hidden = lax.all_gather(grad_share, 'tp', axis=1, tiled=True)  86.8 us
    all_to_all x4, other arithmetic, side_by_side(): lax.all_to_all(both, axis, split_axis=split_dim, concat_axis=concat_dim,...  29.8 us
  transfers between devices with their start and end apart: 3, of which 3 were waited for; matrix products, arithmetic and copies ran while one was open for 3% of the time, Pallas kernels for 0%

commit v1 on v0

--- a/solution.py
+++ b/solution.py
@@ -2,6 +2,13 @@
 import jax.numpy as jnp
 from jax import lax
 from jax.sharding import PartitionSpec as P
+
+
+def all_by_exchange(x, axis, dim):
+    size = lax.axis_size(axis)
+    blocks = jnp.stack([x for _ in range(size)])
+    blocks = lax.all_to_all(blocks, axis, split_axis=0, concat_axis=0)
+    return jnp.concatenate(blocks, axis=dim)
 
 
 def side_by_side(arrays, axis, split_dim, concat_dim, along):
@@ -53,7 +60,7 @@
         partial_value.astype(jnp.bfloat16), "tp", scatter_dimension=1, tiled=True
     ).astype(jnp.float32)
     activation, grad_share = activate(hidden_share, cotangent[0])
-    grad_hidden = lax.all_gather(grad_share, "tp", axis=1, tiled=True)
+    grad_hidden = all_by_exchange(grad_share, "tp", 1)
     grad_weight = lax.dot_general(
         inputs, grad_hidden, (((0,), (0,)), ((), ())), preferred_element_type=jnp.float32
     )

time: 710 us -> 734 us (1.034)
  the two profiles are of different devices: /device:TPU:1 before, /device:TPU:6 now
where the time goes in v1:
time: 734 us; the launch traced here: 725 us
  waiting for transfers between devices  342 us (47%)
  blocking collectives  149 us (20%)
  local copies, waits for them, and re-layouts  138 us (19%)
  other arithmetic  51.5 us (7%)
  starting transfers between devices  16.3 us (2%)
  matrix products  14.7 us (2%)
  between operations  14.3 us (2%)
    all_to_all x1, blocking collectives, side_by_side(): lax.all_to_all(both, axis, split_axis=split_dim, concat_axis=concat_dim,...  149 us
    all_to_all x1, waiting for transfers between devices, side_by_side(): lax.all_to_all(both, axis, split_axis=split_dim, concat_axis=concat_dim,...  144 us
    reduce_scatter x1, waiting for transfers between devices, local(): lax.psum_scatter(partial_value.astype(jnp.bfloat16), 'tp', scatter_dimens...  104 us
    all_to_all x1, waiting for transfers between devices, all_by_exchange(): blocks = lax.all_to_all(blocks, axis, split_axis=0, concat_axis=0)  93.8 us
    unnamed x16, local copies, waits for them, and re-layouts  87.1 us
    all_to_all x4, other arithmetic, side_by_side(): lax.all_to_all(both, axis, split_axis=split_dim, concat_axis=concat_dim,...  40.4 us
  transfers between devices with their start and end apart: 3, of which 3 were waited for; matrix products, arithmetic and copies ran while one was open for 2% of the time, Pallas kernels for 0%

profile of v1, /device:TPU:6, one launch (start us, length us, event | category | flops | bytes accessed | tf_op | source)
XLA Modules:
  0.0 725.5 jit_solution(15653533331914912755)
XLA Ops:
  7.2 0.0 copy-start
  7.2 5.6 reshape.54
  12.8 6.7 reshape.53
  19.5 5.0 maximum_bitcast_fusion
  24.5 0.5 broadcast.63
  25.0 9.3 %reduce = bf16[32,100352]{1,0:T(8,128)(2,1)} reduce(bf16[32,1,100352]{2,0,1:T(8,128)(2,1)} %maximum_bitcast_fusion, bf16[]{:T(256)} %broadcast.63), dimensions={1}, to_apply=%copy.21.reduce_sub_computation | reduce | bytes 12845058 | tf_op jit(solution)/shard_map/all_to_all | solution.py:17
  34.4 8.9 %reshape.74 = bf16[32,2,50176]{2,1,0:T(2,128)(2,1)} reshape(bf16[32,100352]{1,0:T(8,128)(2,1)} %reduce) | data formatting | bytes 12845056
  43.2 0.0 copy-start.1
  43.2 10.1 %all-to-all-start = ((bf16[32,2,50176]{2,1,0:T(2,128)(2,1)}), bf16[32,2,50176]{2,1,0:T(2,128)(2,1)}, u32[]{:S(2)}, u32[]{:S(2)}) async-start(bf16[32,2,50176]{2,1,0:T(2,128)(2,1)} %reshape.74), calls=%async_computation | async-start | bytes 12845056 | tf_op jit(solution)/shard_map/all_to_all | solution.py:17
  53.3 0.0 reduce-scatter.2.cloned.1.call-start
  53.4 0.0 copy-done.1
  53.4 0.1 fusion.20
  53.5 0.1 select_reduce_fusion
  53.6 144.2 %all-to-all-done = bf16[32,2,50176]{2,1,0:T(2,128)(2,1)} async-done(((bf16[32,2,50176]{2,1,0:T(2,128)(2,1)}), bf16[32,2,50176]{2,1,0:T(2,128)(2,1)}, u32[]{:S(2)}, u32[]{:S(2)}) %all-to-all-start) | async-done | bytes 6422560 | tf_op jit(solution)/shard_map/all_to_all | solution.py:17
  197.8 21.7 %reshape.75 = bf16[32,1,100352]{2,1,0:T(2,128)(2,1)} reshape(bf16[32,2,50176]{2,1,0:T(2,128)(2,1)} %all-to-all-done) | data formatting | bytes 12845056
  219.5 11.0 %copy.30 = bf16[32,1,100352]{2,0,1:T(8,128)(2,1)} copy(bf16[32,1,100352]{2,1,0:T(2,128)(2,1)} %reshape.75) | data formatting | bytes 12845056
  230.5 5.0 fusion.24
  235.5 9.4 %gather_fusion.1 = bf16[32,50176]{1,0:T(8,128)(2,1)} fusion(bf16[32,50176]{1,0:T(8,128)(2,1)} %get-tuple-element.13, s32[1024]{0:T(1024)S(1)} %pad_clamp_fusion), kind=kCustom, calls=%fused_computation.1 | custom fusion | bytes 6422656 | tf_op jit(solution)/shard_map/gather | solution.py:53
  244.8 4.3 gather_fusion
  249.2 6.0 maximum_bitcast_fusion.1
  255.2 20.1 %reduce.1 = bf16[32,100352]{1,0:T(8,128)(2,1)} reduce(bf16[32,1,100352]{2,0,1:T(8,128)(2,1)} %maximum_bitcast_fusion.1, bf16[]{:T(256)} %broadcast.63), dimensions={1}, to_apply=%copy.22.reduce_sub_computation | reduce | bytes 12845058 | tf_op jit(solution)/shard_map/all_to_all | solution.py:17
  275.3 8.9 %reshape.76 = bf16[32,2,50176]{2,1,0:T(2,128)(2,1)} reshape(bf16[32,100352]{1,0:T(8,128)(2,1)} %reduce.1) | data formatting | bytes 12845056
  284.1 149.2 %all_to_all.29 = bf16[32,2,50176]{2,1,0:T(2,128)(2,1)} all-to-all(bf16[32,2,50176]{2,1,0:T(2,128)(2,1)} %reshape.76), channel_id=1, replica_groups=mesh['pop'=32,'tp'=8] {'pop'}, dimensions={0} | all-to-all | bytes 12845056 | tf_op jit(solution)/shard_map/all_to_all | solution.py:17
  433.4 21.3 %reshape.77 = bf16[32,1,100352]{2,1,0:T(2,128)(2,1)} reshape(bf16[32,2,50176]{2,1,0:T(2,128)(2,1)} %all_to_all.29) | data formatting | bytes 12845056
  454.7 11.0 %copy.29 = bf16[32,1,100352]{2,0,1:T(8,128)(2,1)} copy(bf16[32,1,100352]{2,1,0:T(2,128)(2,1)} %reshape.77) | data formatting | bytes 12845056
  465.7 3.8 slice.30
  469.5 5.5 squeeze_reshape.4
  475.0 0.0 copy-done
  475.0 5.1 fusion
  480.1 0.0 copy-start.2
  480.1 0.0 copy-start.3
  480.1 0.0 reduce-scatter.2.cloned.1.call-update
  480.1 2.2 copy.23
  482.3 0.0 copy-done.2
  482.3 0.6 fusion.21
  483.0 0.0 copy-done.3
  483.0 1.3 fusion.22
  484.3 103.6 %reduce-scatter.2.cloned.1.call-done = bf16[512,896]{0,1:T(8,128)(2,1)} async-done(((bf16[512,7168]{0,1:T(8,128)(2,1)}), bf16[512,896]{0,1:T(8,128)(2,1)}) %reduce-scatter.2.cloned.1.call-update) | async-done | bytes 917520 | tf_op jit(solution)/shard_map/reduce_scatter | solution.py:59
  587.9 3.8 fusion.9
  591.7 3.7 stack.2
  595.4 6.2 all-to-all-start.2
  601.5 5.1 convert_multiply_fusion
  606.6 6.2 mul.66
  612.8 2.2 copy.24
  615.0 93.8 %all-to-all-done.2 = bf16[8,512,896]{1,2,0:T(8,128)(2,1)} async-done(((bf16[8,512,896]{1,2,0:T(8,128)(2,1)}), bf16[8,512,896]{1,2,0:T(8,128)(2,1)}, u32[]{:S(2)}, u32[]{:S(2)}) %all-to-all-start.2) | async-done | bytes 7340064 | tf_op jit(solution)/shard_map/all_to_all | solution.py:10
  708.8 9.7 %fusion.5 = bf16[1,224,7168]{2,1,0:T(8,128)(2,1)} fusion(f32[224,7168]{1,0:T(8,128)} %mul.66, bf16[512,7168]{0,1:T(8,128)(2,1)} %bitcast.13, bf16[224,7168]{1,0:T(8,128)(2,1)S(1)} %squeeze_reshape.4, f32[]{:T(128)} %fusion.22, bf16[1,512,224]{1,2,0:T(8,128)(2,1)S(1)} %copy-done), kind=kOutput, calls=%fused_computation.9 | convolution fusion | flops 1652195328 | bytes 20414468 | tf_op jit(solution)/shard_map/dot_general | solution.py:64
  (3 shorter events, 0.0 us)
Async XLA Ops:
  7.2 467.8 %copy-start = (bf16[1,512,224]{1,2,0:T(8,128)(2,1)S(1)}, bf16[1,512,224]{1,2,0:T(8,128)(2,1)}, u32[]{:S(2)}) copy-start(bf16[1,512,224]{1,2,0:T(8,128)(2,1)} %param.7) | copy-start | bytes 688132
  43.2 10.2 %copy-start.1 = (s32[8,2]{0,1:T(2,128)S(1)}, s32[8,2]{0,1:T(2,128)}, u32[]{:S(2)}) copy-start(s32[8,2]{0,1:T(2,128)} %param.11) | copy-start | bytes 196
  43.2 154.6 %all-to-all-start = ((bf16[32,2,50176]{2,1,0:T(2,128)(2,1)}), bf16[32,2,50176]{2,1,0:T(2,128)(2,1)}, u32[]{:S(2)}, u32[]{:S(2)}) async-start(bf16[32,2,50176]{2,1,0:T(2,128)(2,1)} %reshape.74), calls=%async_computation | async-start | bytes 12845056 | tf_op jit(solution)/shard_map/all_to_all | solution.py:17
  53.3 534.5 %reduce-scatter.2.cloned.1.call-start = ((), (), s32[]{:S(2)}) async-start(), calls=%async_computation.4 | async-start | bytes 8257536 | tf_op jit(solution)/shard_map/reduce_scatter | solution.py:59
  480.1 2.3 copy-start.2
  480.1 2.9 copy-start.3
  595.4 113.4 %all-to-all-start.2 = ((bf16[8,512,896]{1,2,0:T(8,128)(2,1)}), bf16[8,512,896]{1,2,0:T(8,128)(2,1)}, u32[]{:S(2)}, u32[]{:S(2)}) async-start(bf16[8,512,896]{1,2,0:T(8,128)(2,1)} %stack.2), calls=%async_computation.3 | async-start | bytes 14680064 | tf_op jit(solution)/shard_map/all_to_all | solution.py:10
Sparse Core Ops, SparseCore 0:
  480.2 107.5 reduce-scatter.1
